TPU v7x, 32 devices: a whole 2x2x4 slice. The times are simulated.
32 devices in a mesh: dp: 8 (over y, x, core), seq: 4 (over z).
Axes of the slice: x: 2, y: 2, z: 4, core: 2. Of those that a mesh axis runs over, the one named last changes fastest.
Arguments:
- img_q_raw: bfloat16 [8, 512, 1536], P('dp', 'seq'), may hold values from -12 to 12
- img_k_raw: bfloat16 [8, 512, 1536], P('dp', 'seq'), may hold values from -6 to 6
- img_v: bfloat16 [8, 512, 1536], P('dp', 'seq'), may hold values from -6 to 6
- img_dout: bfloat16 [8, 512, 1536], P('dp', 'seq'), may hold values from -6 to 6
- txt_q_raw: bfloat16 [8, 64, 1536], P('dp', 'seq'), may hold values from -6 to 6
- txt_k_raw: bfloat16 [8, 64, 1536], P('dp'), may hold values from -6 to 6
- txt_v: bfloat16 [8, 64, 1536], P('dp'), may hold values from -6 to 6
- txt_dout: bfloat16 [8, 64, 1536], P('dp', 'seq'), may hold values from -6 to 6
- q_gain: float32 [128], replicated, may hold values from 0.6 to 3.8
- k_gain: float32 [128], replicated, may hold values from 0.6 to 3.8
Outputs:
- img_dq: bfloat16 [8, 512, 1536], P('dp', 'seq')
- img_dk: bfloat16 [8, 512, 1536], P('dp', 'seq')
- img_dv: bfloat16 [8, 512, 1536], P('dp', 'seq')
- txt_dq: bfloat16 [8, 64, 1536], P('dp', 'seq')
- txt_dk: bfloat16 [8, 64, 1536], P('dp', 'seq')
- txt_dv: bfloat16 [8, 64, 1536], P('dp', 'seq')
- q_gain_grad: float32 [128], replicated
- k_gain_grad: float32 [128], replicated
All inputs are finite; a program needn't handle non-finite values.
Results may differ from a plain program's by a relative error of at most 0.012.
The roundings to bfloat16 on the way count: a program that leaves them out, or rounds other values in their place, can miss the bound.
Values may be sent and summed in bfloat16 or wider, within the bound.
A program may use at most 64 MiB of HBM per device.

v0:
```python
import jax
import jax.numpy as jnp
from jax import lax
from jax.sharding import PartitionSpec as P

HEAD_DIM = 128


epsilon = 1e-06


def normalize(source, norm_gain):
    values = source.astype(jnp.float32)
    inverse = lax.rsqrt(jnp.mean(values * values, axis=-1, keepdims=True) + epsilon)
    return values * inverse * norm_gain


def norm_backward(source, norm_gain, upstream):
    values = source.astype(jnp.float32)
    result_value, pullback = jax.vjp(normalize, values, norm_gain)
    return pullback(upstream)


def group_back(operands):
    query_b, key_b, value_all, dout_blocks = operands
    score_scale = query_b.shape[-1] ** (-0.5)
    scores = (
        jnp.einsum("nqhd,khd->nhqk", query_b, key_b, preferred_element_type=jnp.float32)
        * score_scale
    )
    row_max = jnp.max(scores, axis=-1, keepdims=True)
    shifted = scores - row_max
    log_total = jnp.log(jnp.sum(jnp.exp(shifted), axis=-1, keepdims=True))
    prob_full = jnp.exp(shifted - log_total)
    probs_b = prob_full.astype(jnp.bfloat16)
    output_b = jnp.einsum(
        "nhqk,khd->nqhd", probs_b, value_all, preferred_element_type=jnp.float32
    ).astype(jnp.bfloat16)
    output_b = lax.optimization_barrier(output_b)
    dprob = jnp.einsum("nqhd,khd->nhqk", dout_blocks, value_all, preferred_element_type=jnp.float32)
    row_delta = jnp.sum(dout_blocks.astype(jnp.float32) * output_b.astype(jnp.float32), axis=-1)
    row_delta = jnp.transpose(row_delta, (0, 2, 1))[..., None]
    dscore_b = (prob_full * (dprob - row_delta) * score_scale).astype(jnp.bfloat16)
    dquery = jnp.einsum("nhqk,khd->nqhd", dscore_b, key_b, preferred_element_type=jnp.float32)
    key_terms = jnp.einsum("nhqk,nqhd->nkhd", dscore_b, query_b, preferred_element_type=jnp.float32)
    value_terms = jnp.einsum(
        "nhqk,nqhd->nkhd", probs_b, dout_blocks, preferred_element_type=jnp.float32
    )
    return (dquery, key_terms, value_terms)


def forward_back(query_b, key_b, value_all, dout_blocks):
    block_count, query_rows, heads_here, feature_count = query_b.shape
    key_rows = key_b.shape[0]
    group_count = heads_here // heads_here

    def split_rows(source):
        return jnp.moveaxis(
            source.reshape(block_count, query_rows, group_count, heads_here, feature_count), 2, 0
        )

    def split_keys(source):
        return jnp.moveaxis(source.reshape(key_rows, group_count, heads_here, feature_count), 1, 0)

    dquery_g, key_g, value_g = lax.map(
        group_back,
        (split_rows(query_b), split_keys(key_b), split_keys(value_all), split_rows(dout_blocks)),
    )
    dquery = jnp.moveaxis(dquery_g, 0, 2).reshape(
        block_count, query_rows, heads_here, feature_count
    )
    key_terms = jnp.moveaxis(key_g, 0, 2).reshape(block_count, key_rows, heads_here, feature_count)
    value_terms = jnp.moveaxis(value_g, 0, 2).reshape(
        block_count, key_rows, heads_here, feature_count
    )
    return (dquery, key_terms, value_terms)


def local(
    img_q_raw, img_k_raw, img_v, img_dout, txt_q_raw, txt_k_raw, txt_v, txt_dout, q_gain, k_gain
):
    seq_count = lax.axis_size("seq")
    my_index = lax.axis_index("seq")
    image_q = img_q_raw[0]
    image_k = img_k_raw[0]
    image_v = img_v[0]
    image_d = img_dout[0]
    text_q = txt_q_raw[0]
    text_k = txt_k_raw[0]
    text_v = txt_v[0]
    text_d = txt_dout[0]
    lane_width = image_q.shape[1]
    head_count = lane_width // HEAD_DIM
    img_rows = image_q.shape[0]
    text_rows = text_q.shape[0]
    text_all = text_k.shape[0]
    image_total = img_rows * seq_count
    exchanged = (
        lax.all_to_all(image_q, "seq", split_axis=1, concat_axis=0, tiled=True),
        lax.all_to_all(image_k, "seq", split_axis=1, concat_axis=0, tiled=True),
        lax.all_to_all(image_v, "seq", split_axis=1, concat_axis=0, tiled=True),
        lax.all_to_all(image_d, "seq", split_axis=1, concat_axis=0, tiled=True),
        lax.all_to_all(text_q, "seq", split_axis=1, concat_axis=0, tiled=True),
        lax.all_to_all(text_d, "seq", split_axis=1, concat_axis=0, tiled=True),
    )
    moved_iq, moved_ik, moved_iv, moved_id, moved_tq, moved_td = exchanged
    local_heads = head_count // seq_count
    head_lanes = local_heads * HEAD_DIM
    key_text = lax.dynamic_slice_in_dim(text_k, my_index * head_lanes, head_lanes, 1)
    value_text = lax.dynamic_slice_in_dim(text_v, my_index * head_lanes, head_lanes, 1)
    query_src = jnp.concatenate(
        [
            moved_iq.reshape(seq_count, img_rows, local_heads, HEAD_DIM),
            moved_tq.reshape(seq_count, text_rows, local_heads, HEAD_DIM),
        ],
        axis=1,
    )
    dout_blocks = jnp.concatenate(
        [
            moved_id.reshape(seq_count, img_rows, local_heads, HEAD_DIM),
            moved_td.reshape(seq_count, text_rows, local_heads, HEAD_DIM),
        ],
        axis=1,
    )
    key_src = jnp.concatenate([moved_ik, key_text], axis=0).reshape(
        image_total + text_all, local_heads, HEAD_DIM
    )
    value_all = jnp.concatenate([moved_iv, value_text], axis=0).reshape(
        image_total + text_all, local_heads, HEAD_DIM
    )
    query_b = normalize(query_src, q_gain).astype(jnp.bfloat16)
    key_b = normalize(key_src, k_gain).astype(jnp.bfloat16)
    dquery, key_f, value_f = forward_back(query_b, key_b, value_all, dout_blocks)
    key_terms = key_f.astype(jnp.bfloat16)
    value_terms = value_f.astype(jnp.bfloat16)
    key_terms, value_terms = lax.optimization_barrier((key_terms, value_terms))
    dkey = jnp.sum(key_terms.astype(jnp.float32), axis=0)
    dvalue = jnp.sum(value_terms.astype(jnp.float32), axis=0)
    dquery_src, dq_gain = norm_backward(query_src, q_gain, dquery)
    dkey_src, dk_gain = norm_backward(key_src, k_gain, dkey)
    dq_b = dquery_src.astype(jnp.bfloat16)
    dk_b = dkey_src.reshape(image_total + text_all, head_lanes).astype(jnp.bfloat16)
    dv_b = dvalue.reshape(image_total + text_all, head_lanes).astype(jnp.bfloat16)
    returned = (
        dq_b[:, :img_rows].reshape(image_total, head_lanes),
        dk_b[:image_total],
        dv_b[:image_total],
        dq_b[:, img_rows:].reshape(text_all, head_lanes),
        dk_b[image_total:],
        dv_b[image_total:],
    )
    grad_iq, grad_ik, grad_iv, grad_tq, grad_tk, grad_tv = (
        lax.all_to_all(returned[0], "seq", split_axis=0, concat_axis=1, tiled=True),
        lax.all_to_all(returned[1], "seq", split_axis=0, concat_axis=1, tiled=True),
        lax.all_to_all(returned[2], "seq", split_axis=0, concat_axis=1, tiled=True),
        lax.all_to_all(returned[3], "seq", split_axis=0, concat_axis=1, tiled=True),
        lax.all_to_all(returned[4], "seq", split_axis=0, concat_axis=1, tiled=True),
        lax.all_to_all(returned[5], "seq", split_axis=0, concat_axis=1, tiled=True),
    )
    gain_q, gain_k = lax.psum((dq_gain, dk_gain), ("dp", "seq"))
    return (
        grad_iq[None],
        grad_ik[None],
        grad_iv[None],
        grad_tq[None],
        grad_tk[None],
        grad_tv[None],
        gain_q,
        gain_k,
    )


def solution(mesh):
    return jax.shard_map(
        local,
        mesh=mesh,
        in_specs=(
            P("dp", "seq", None),
            P("dp", "seq", None),
            P("dp", "seq", None),
            P("dp", "seq", None),
            P("dp", "seq", None),
            P("dp", None, None),
            P("dp", None, None),
            P("dp", "seq", None),
            P(),
            P(),
        ),
        out_specs=(
            P("dp", "seq", None),
            P("dp", "seq", None),
            P("dp", "seq", None),
            P("dp", "seq", None),
            P("dp", "seq", None),
            P("dp", "seq", None),
            P(),
            P(),
        ),
        check_vma=False,
    )
```

profile of v0, /device:TPU:0, one launch (start us, length us, event | category | flops | bytes accessed | tf_op | source)
XLA Modules:
  0.0 206.6 jit_solution(5955745471128264303)
XLA Ops:
  2.2 6.3 %all-to-all-start.2 = ((bf16[16,4,384]{2,0,1:T(8,128)(2,1)}), bf16[16,4,384]{2,0,1:T(8,128)(2,1)S(1)}, u32[]{:S(2)}, u32[]{:S(2)}) async-start(bf16[16,4,384]{2,0,1:T(8,128)(2,1)} %copy.91), calls=%async_computation.2 | async-start | bytes 98304 | tf_op jit(solution)/shard_map/all_to_all | solution.py:103
  9.9 4.3 %all-to-all-done.2 = bf16[16,4,384]{2,0,1:T(8,128)(2,1)S(1)} async-done(((bf16[16,4,384]{2,0,1:T(8,128)(2,1)}), bf16[16,4,384]{2,0,1:T(8,128)(2,1)S(1)}, u32[]{:S(2)}, u32[]{:S(2)}) %all-to-all-start.2) | async-done | bytes 49184 | tf_op jit(solution)/shard_map/all_to_all | solution.py:103
  14.2 3.3 %all-to-all-start.5 = ((bf16[16,4,384]{2,0,1:T(8,128)(2,1)}), bf16[16,4,384]{2,0,1:T(8,128)(2,1)S(1)}, u32[]{:S(2)}, u32[]{:S(2)}) async-start(bf16[16,4,384]{2,0,1:T(8,128)(2,1)} %copy.99), calls=%async_computation.5 | async-start | bytes 98304 | tf_op jit(solution)/shard_map/all_to_all | solution.py:104
  17.5 1.9 copy.86
  19.4 3.8 %all-to-all-done.5 = bf16[16,4,384]{2,0,1:T(8,128)(2,1)S(1)} async-done(((bf16[16,4,384]{2,0,1:T(8,128)(2,1)}), bf16[16,4,384]{2,0,1:T(8,128)(2,1)S(1)}, u32[]{:S(2)}, u32[]{:S(2)}) %all-to-all-start.5) | async-done | bytes 49184 | tf_op jit(solution)/shard_map/all_to_all | solution.py:104
  23.1 3.5 %all-to-all-start = ((bf16[128,4,384]{0,2,1:T(8,128)(2,1)}), bf16[128,4,384]{0,2,1:T(8,128)(2,1)S(1)}, u32[]{:S(2)}, u32[]{:S(2)}) async-start(bf16[128,4,384]{0,2,1:T(8,128)(2,1)} %bitcast), calls=%async_computation | async-start | bytes 786432 | tf_op jit(solution)/shard_map/all_to_all | solution.py:100
  28.3 1.9 copy.90
  30.8 1.9 copy.94
  33.7 2.3 %all-to-all-done = bf16[128,4,384]{0,2,1:T(8,128)(2,1)S(1)} async-done(((bf16[128,4,384]{0,2,1:T(8,128)(2,1)}), bf16[128,4,384]{0,2,1:T(8,128)(2,1)S(1)}, u32[]{:S(2)}, u32[]{:S(2)}) %all-to-all-start) | async-done | bytes 393248 | tf_op jit(solution)/shard_map/all_to_all | solution.py:100
  36.0 3.5 %all-to-all-start.1 = ((bf16[128,4,384]{0,2,1:T(8,128)(2,1)}), bf16[128,4,384]{0,2,1:T(8,128)(2,1)S(1)}, u32[]{:S(2)}, u32[]{:S(2)}) async-start(bf16[128,4,384]{0,2,1:T(8,128)(2,1)} %bitcast.4), calls=%async_computation.1 | async-start | bytes 786432 | tf_op jit(solution)/shard_map/all_to_all | solution.py:99
  40.2 8.6 %all-to-all-done.1 = bf16[128,4,384]{0,2,1:T(8,128)(2,1)S(1)} async-done(((bf16[128,4,384]{0,2,1:T(8,128)(2,1)}), bf16[128,4,384]{0,2,1:T(8,128)(2,1)S(1)}, u32[]{:S(2)}, u32[]{:S(2)}) %all-to-all-start.1) | async-done | bytes 393248 | tf_op jit(solution)/shard_map/all_to_all | solution.py:99
  48.7 3.5 %all-to-all-start.3 = ((bf16[128,4,384]{0,2,1:T(8,128)(2,1)}), bf16[128,4,384]{0,2,1:T(8,128)(2,1)S(1)}, u32[]{:S(2)}, u32[]{:S(2)}) async-start(bf16[128,4,384]{0,2,1:T(8,128)(2,1)} %bitcast.12), calls=%async_computation.3 | async-start | bytes 786432 | tf_op jit(solution)/shard_map/all_to_all | solution.py:101
  54.5 2.9 %fusion.39 = f32[3,576,576]{1,2,0} fusion(bf16[3,128,576]{1,2,0:T(8,128)(2,1)S(1)} %bitcast.111, f32[128]{0:T(128)S(1)} %copy-done.15, f32[576,3]{0,1:T(4,128)S(1)} %fusion.43, bf16[64,3,128]{2,0,1:T(8,128)(2,1)S(1)} %copy.89, bf16[512,3,128]{2,0,1:T(8,128)(2,1)S(1)} %copy.88), kind=kOutput, calls=%fused_computation.57 | convolution fusion | flops 256352256 | bytes 4873472
  57.3 4.2 %all-to-all-done.3 = bf16[128,4,384]{0,2,1:T(8,128)(2,1)S(1)} async-done(((bf16[128,4,384]{0,2,1:T(8,128)(2,1)}), bf16[128,4,384]{0,2,1:T(8,128)(2,1)S(1)}, u32[]{:S(2)}, u32[]{:S(2)}) %all-to-all-start.3) | async-done | bytes 393248 | tf_op jit(solution)/shard_map/all_to_all | solution.py:101
  61.5 3.6 %all-to-all-start.4 = ((bf16[128,4,384]{0,2,1:T(8,128)(2,1)}), bf16[128,4,384]{0,2,1:T(8,128)(2,1)S(1)}, u32[]{:S(2)}, u32[]{:S(2)}) async-start(bf16[128,4,384]{0,2,1:T(8,128)(2,1)} %bitcast.14), calls=%async_computation.4 | async-start | bytes 786432 | tf_op jit(solution)/shard_map/all_to_all | solution.py:102
  65.2 6.4 %bitcast_subtract_fusion = f32[4,3,144,576]{3,2,0,1:T(8,128)} fusion(f32[3,576,4,144]{1,3,2,0:T(8,128)} %bitcast.107), kind=kOutput, calls=%fused_computation.5 | output fusion | flops 2988287 | bytes 7962624 | tf_op jit(solution)/shard_map/while/body/eval_jaxpr/sub | solution.py:32
  72.9 7.0 %fusion.47 = (bf16[4,3,144,576]{3,2,0,1:T(8,128)(2,1)S(1)}, f32[4,3,144,576]{3,2,0,1:T(8,128)}) fusion(f32[4,3,144,576]{3,2,0,1:T(8,128)} %bitcast_subtract_fusion), kind=kOutput, calls=%fused_computation.75 | output fusion | flops 1992959 | bytes 9953280 | tf_op jit(solution)/shard_map/while/body/eval_jaxpr/reduce_sum | solution.py:33
  82.0 2.5 %convert_bitcast_fusion = bf16[4,576,3,128]{3,1,2,0:T(8,128)(2,1)} fusion(bf16[4,3,144,576]{3,2,0,1:T(8,128)(2,1)S(1)} %get-tuple-element.66, bf16[4,16,3,128]{3,1,0,2:T(8,128)(2,1)S(1)} %copy_bitcast_fusion.1, bf16[4,128,3,128]{3,1,0,2:T(8,128)(2,1)S(1)} %copy.100), kind=kOutput, calls=%fused_computation.17 | convolution fusion | flops 256573440 | bytes 4202496 | tf_op jit(solution)/shard_map/while/body/eval_jaxpr/nhqk,nqhd->nkhd/dot_general | solution.py:46
  88.8 2.5 %fusion.26 = (f32[128]{0:T(128)}, f32[4,144,3]{1,0,2:T(4,128)}, f32[4,144,3,128]{3,1,0,2:T(8,128)}) fusion(f32[4,144,3]{1,0,2:T(4,128)S(1)} %copy-done.11, bf16[4,16,3,128]{3,1,0,2:T(8,128)(2,1)S(1)} %copy_bitcast_fusion.2, bf16[4,128,3,128]{3,1,0,2:T(8,128)(2,1)S(1)} %copy.92, f32[128]{0:T(128)S(1)} %copy-done.18, ...), kind=kOutput, calls=%fused_computation.40 | convolution fusion | flops 258562240 | bytes 3782400 | tf_op jit(solution)/shard_map/while/body/eval_jaxpr/nhqk,khd->nqhd/dot_general | solution.py:44
  98.4 4.9 %all-to-all-start.10 = ((bf16[4,16,384]{2,1,0:T(8,128)(2,1)}), bf16[4,16,384]{2,1,0:T(8,128)(2,1)S(1)}, u32[]{:S(2)}, u32[]{:S(2)}) async-start(bf16[4,16,384]{2,1,0:T(8,128)(2,1)} %bitcast.44), calls=%async_computation.10 | async-start | bytes 98304 | tf_op jit(solution)/shard_map/all_to_all | solution.py:157
  104.0 1.7 fusion.31
  107.0 2.0 all-to-all-done.10
  109.0 3.5 %all-to-all-start.11 = ((bf16[4,16,384]{2,1,0:T(8,128)(2,1)}), bf16[4,16,384]{2,1,0:T(8,128)(2,1)S(1)}, u32[]{:S(2)}, u32[]{:S(2)}) async-start(bf16[4,16,384]{2,1,0:T(8,128)(2,1)} %all_to_all.177), calls=%async_computation.11 | async-start | bytes 98304 | tf_op jit(solution)/shard_map/all_to_all | solution.py:158
  113.2 5.0 %all-to-all-done.11 = bf16[4,16,384]{2,1,0:T(8,128)(2,1)S(1)} async-done(((bf16[4,16,384]{2,1,0:T(8,128)(2,1)}), bf16[4,16,384]{2,1,0:T(8,128)(2,1)S(1)}, u32[]{:S(2)}, u32[]{:S(2)}) %all-to-all-start.11) | async-done | bytes 49184 | tf_op jit(solution)/shard_map/all_to_all | solution.py:158
  118.2 3.3 %all-to-all-start.9 = ((bf16[4,16,384]{2,1,0:T(8,128)(2,1)}), bf16[4,16,384]{2,1,0:T(8,128)(2,1)S(1)}, u32[]{:S(2)}, u32[]{:S(2)}) async-start(bf16[4,16,384]{2,1,0:T(8,128)(2,1)} %copy_bitcast_fusion), calls=%async_computation.9 | async-start | bytes 98304 | tf_op jit(solution)/shard_map/all_to_all | solution.py:156
  122.4 4.8 %all-to-all-done.9 = bf16[4,16,384]{2,1,0:T(8,128)(2,1)S(1)} async-done(((bf16[4,16,384]{2,1,0:T(8,128)(2,1)}), bf16[4,16,384]{2,1,0:T(8,128)(2,1)S(1)}, u32[]{:S(2)}, u32[]{:S(2)}) %all-to-all-start.9) | async-done | bytes 49184 | tf_op jit(solution)/shard_map/all_to_all | solution.py:156
  127.2 3.5 %all-to-all-start.7 = ((bf16[4,128,384]{2,1,0:T(8,128)(2,1)}), bf16[4,128,384]{2,1,0:T(8,128)(2,1)S(1)}, u32[]{:S(2)}, u32[]{:S(2)}) async-start(bf16[4,128,384]{2,1,0:T(8,128)(2,1)} %bitcast.38), calls=%async_computation.7 | async-start | bytes 786432 | tf_op jit(solution)/shard_map/all_to_all | solution.py:154
  131.8 7.7 %all-to-all-done.7 = bf16[4,128,384]{2,1,0:T(8,128)(2,1)S(1)} async-done(((bf16[4,128,384]{2,1,0:T(8,128)(2,1)}), bf16[4,128,384]{2,1,0:T(8,128)(2,1)S(1)}, u32[]{:S(2)}, u32[]{:S(2)}) %all-to-all-start.7) | async-done | bytes 393248 | tf_op jit(solution)/shard_map/all_to_all | solution.py:154
  139.6 5.6 %all-to-all-start.8 = ((bf16[4,128,384]{1,2,0:T(8,128)(2,1)}), bf16[4,128,384]{1,2,0:T(8,128)(2,1)S(1)}, u32[]{:S(2)}, u32[]{:S(2)}) async-start(bf16[4,128,384]{1,2,0:T(8,128)(2,1)} %copy.115), calls=%async_computation.8 | async-start | bytes 786432 | tf_op jit(solution)/shard_map/all_to_all | solution.py:155
  146.1 11.2 %all-to-all-done.8 = bf16[4,128,384]{1,2,0:T(8,128)(2,1)S(1)} async-done(((bf16[4,128,384]{1,2,0:T(8,128)(2,1)}), bf16[4,128,384]{1,2,0:T(8,128)(2,1)S(1)}, u32[]{:S(2)}, u32[]{:S(2)}) %all-to-all-start.8) | async-done | bytes 393248 | tf_op jit(solution)/shard_map/all_to_all | solution.py:155
  157.4 3.5 %all-to-all-start.6 = ((bf16[4,128,384]{1,2,0:T(8,128)(2,1)}), bf16[4,128,384]{1,2,0:T(8,128)(2,1)S(1)}, u32[]{:S(2)}, u32[]{:S(2)}) async-start(bf16[4,128,384]{1,2,0:T(8,128)(2,1)} %bitcast.27), calls=%async_computation.6 | async-start | bytes 786432 | tf_op jit(solution)/shard_map/all_to_all | solution.py:153
  160.8 40.7 %all-reduce = (f32[128]{0:T(128)}, f32[128]{0:T(128)}) all-reduce(f32[128]{0:T(128)S(1)} %copy-done.20, f32[128]{0:T(128)S(1)} %copy-done.19), channel_id=1, replica_groups=mesh['dp'=8,'seq'=4] {'dp','seq'}, use_global_device_ids=true, to_apply=%region_10.11 | all-reduce | flops 256 | bytes 2048 | tf_op jit(solution)/shard_map/psum | solution.py:160
  (115 shorter events, 34.3 us)
Async XLA Ops:
  0.6 32.1 %copy-start.7 = (bf16[1,128,1536]{2,1,0:T(8,128)(2,1)S(1)}, bf16[1,128,1536]{2,1,0:T(8,128)(2,1)}, u32[]{:S(2)}) copy-start(bf16[1,128,1536]{2,1,0:T(8,128)(2,1)} %param.13) | copy-start | bytes 1179652
  0.6 38.8 %copy-start.15 = (f32[128]{0:T(128)S(1)}, f32[128]{0:T(128)}, u32[]{:S(2)}) copy-start(f32[128]{0:T(128)} %param.19) | copy-start | bytes 1540
  2.2 12.0 %all-to-all-start.2 = ((bf16[16,4,384]{2,0,1:T(8,128)(2,1)}), bf16[16,4,384]{2,0,1:T(8,128)(2,1)S(1)}, u32[]{:S(2)}, u32[]{:S(2)}) async-start(bf16[16,4,384]{2,0,1:T(8,128)(2,1)} %copy.91), calls=%async_computation.2 | async-start | bytes 98304 | tf_op jit(solution)/shard_map/all_to_all | solution.py:103
  14.2 8.9 %all-to-all-start.5 = ((bf16[16,4,384]{2,0,1:T(8,128)(2,1)}), bf16[16,4,384]{2,0,1:T(8,128)(2,1)S(1)}, u32[]{:S(2)}, u32[]{:S(2)}) async-start(bf16[16,4,384]{2,0,1:T(8,128)(2,1)} %copy.99), calls=%async_computation.5 | async-start | bytes 98304 | tf_op jit(solution)/shard_map/all_to_all | solution.py:104
  23.1 12.8 %all-to-all-start = ((bf16[128,4,384]{0,2,1:T(8,128)(2,1)}), bf16[128,4,384]{0,2,1:T(8,128)(2,1)S(1)}, u32[]{:S(2)}, u32[]{:S(2)}) async-start(bf16[128,4,384]{0,2,1:T(8,128)(2,1)} %bitcast), calls=%async_computation | async-start | bytes 786432 | tf_op jit(solution)/shard_map/all_to_all | solution.py:100
  27.5 25.9 %copy-start.17 = (f32[128]{0:T(128)S(1)}, f32[128]{0:T(128)}, u32[]{:S(2)}) copy-start(f32[128]{0:T(128)} %param.18) | copy-start | bytes 1540
  36.0 16.3 %copy-start.3 = (bf16[128,4,384]{0,2,1:T(8,128)(2,1)}, bf16[128,4,384]{0,2,1:T(8,128)(2,1)S(1)}, u32[]{:S(2)}) copy-start(bf16[128,4,384]{0,2,1:T(8,128)(2,1)S(1)} %all-to-all-done) | copy-start | bytes 1179652
  36.0 12.8 %all-to-all-start.1 = ((bf16[128,4,384]{0,2,1:T(8,128)(2,1)}), bf16[128,4,384]{0,2,1:T(8,128)(2,1)S(1)}, u32[]{:S(2)}, u32[]{:S(2)}) async-start(bf16[128,4,384]{0,2,1:T(8,128)(2,1)} %bitcast.4), calls=%async_computation.1 | async-start | bytes 786432 | tf_op jit(solution)/shard_map/all_to_all | solution.py:99
  48.7 12.8 %all-to-all-start.3 = ((bf16[128,4,384]{0,2,1:T(8,128)(2,1)}), bf16[128,4,384]{0,2,1:T(8,128)(2,1)S(1)}, u32[]{:S(2)}, u32[]{:S(2)}) async-start(bf16[128,4,384]{0,2,1:T(8,128)(2,1)} %bitcast.12), calls=%async_computation.3 | async-start | bytes 786432 | tf_op jit(solution)/shard_map/all_to_all | solution.py:101
  53.0 18.6 %copy-start.12 = (f32[4,144,3]{1,0,2:T(4,128)}, f32[4,144,3]{1,0,2:T(4,128)S(1)}, u32[]{:S(2)}) copy-start(f32[4,144,3]{1,0,2:T(4,128)S(1)} %fusion.32) | copy-start | bytes 20740
  53.0 18.6 %copy-start.10 = (f32[4,144,3]{1,0,2:T(4,128)}, f32[4,144,3]{1,0,2:T(4,128)S(1)}, u32[]{:S(2)}) copy-start(f32[4,144,3]{1,0,2:T(4,128)S(1)} %fusion.42) | copy-start | bytes 20740
  53.4 18.2 %copy-start.13 = (f32[576,3]{0,1:T(4,128)}, f32[576,3]{0,1:T(4,128)S(1)}, u32[]{:S(2)}) copy-start(f32[576,3]{0,1:T(4,128)S(1)} %fusion.29) | copy-start | bytes 20740
  61.5 18.4 %all-to-all-start.4 = ((bf16[128,4,384]{0,2,1:T(8,128)(2,1)}), bf16[128,4,384]{0,2,1:T(8,128)(2,1)S(1)}, u32[]{:S(2)}, u32[]{:S(2)}) async-start(bf16[128,4,384]{0,2,1:T(8,128)(2,1)} %bitcast.14), calls=%async_computation.4 | async-start | bytes 786432 | tf_op jit(solution)/shard_map/all_to_all | solution.py:102
  81.9 2.6 %copy-start.4 = (bf16[512,3,128]{2,0,1:T(8,128)(2,1)S(1)}, bf16[512,3,128]{2,0,1:T(8,128)(2,1)}, u32[]{:S(2)}) copy-start(bf16[512,3,128]{2,0,1:T(8,128)(2,1)} %copy.96) | copy-start | bytes 1179652
  81.9 2.5 %copy-start.6 = (bf16[64,3,128]{2,0,1:T(8,128)(2,1)S(1)}, bf16[64,3,128]{2,0,1:T(8,128)(2,1)}, u32[]{:S(2)}) copy-start(bf16[64,3,128]{2,0,1:T(8,128)(2,1)} %copy.97) | copy-start | bytes 147460
  82.0 4.5 %slice-start = ((s8[4423680]{0:T(1024)(128)(4,1)}), s8[4194304]{0:T(1024)(128)(4,1)S(1)}, s32[]{:S(2)}) async-start(s8[4423680]{0:T(1024)(128)(4,1)} %bitcast.108), calls=%async_computation.12 | async-start | bytes 8388608
  84.5 2.0 slice-start.1
  87.5 1.3 copy-start.11
  87.5 1.3 copy-start.16
  87.5 1.3 copy-start.18
  91.6 14.2 %copy-start = (bf16[4,576,3,128]{3,1,2,0:T(8,128)(2,1)S(1)}, bf16[4,576,3,128]{3,1,2,0:T(8,128)(2,1)}, u32[]{:S(2)}) copy-start(bf16[4,576,3,128]{3,1,2,0:T(8,128)(2,1)} %convert_bitcast_fusion) | copy-start | bytes 5308420
  92.8 10.5 %copy-start.14 = (f32[4,144,3]{1,0,2:T(4,128)S(1)}, f32[4,144,3]{1,0,2:T(4,128)}, u32[]{:S(2)}) copy-start(f32[4,144,3]{1,0,2:T(4,128)} %get-tuple-element.63) | copy-start | bytes 20740
  98.4 10.6 %all-to-all-start.10 = ((bf16[4,16,384]{2,1,0:T(8,128)(2,1)}), bf16[4,16,384]{2,1,0:T(8,128)(2,1)S(1)}, u32[]{:S(2)}, u32[]{:S(2)}) async-start(bf16[4,16,384]{2,1,0:T(8,128)(2,1)} %bitcast.44), calls=%async_computation.10 | async-start | bytes 98304 | tf_op jit(solution)/shard_map/all_to_all | solution.py:157
  109.0 9.2 %copy-start.8 = (bf16[4,16,384]{2,1,0:T(8,128)(2,1)}, bf16[4,16,384]{2,1,0:T(8,128)(2,1)S(1)}, u32[]{:S(2)}) copy-start(bf16[4,16,384]{2,1,0:T(8,128)(2,1)S(1)} %all-to-all-done.10) | copy-start | bytes 147460
  109.0 9.2 %all-to-all-start.11 = ((bf16[4,16,384]{2,1,0:T(8,128)(2,1)}), bf16[4,16,384]{2,1,0:T(8,128)(2,1)S(1)}, u32[]{:S(2)}, u32[]{:S(2)}) async-start(bf16[4,16,384]{2,1,0:T(8,128)(2,1)} %all_to_all.177), calls=%async_computation.11 | async-start | bytes 98304 | tf_op jit(solution)/shard_map/all_to_all | solution.py:158
  112.5 48.3 %copy-start.19 = (f32[128]{0:T(128)S(1)}, f32[128]{0:T(128)}, u32[]{:S(2)}) copy-start(f32[128]{0:T(128)} %get-tuple-element.60) | copy-start | bytes 1540
  112.5 48.3 %copy-start.20 = (f32[128]{0:T(128)S(1)}, f32[128]{0:T(128)}, u32[]{:S(2)}) copy-start(f32[128]{0:T(128)} %get-tuple-element.62) | copy-start | bytes 1540
  118.2 9.1 %all-to-all-start.9 = ((bf16[4,16,384]{2,1,0:T(8,128)(2,1)}), bf16[4,16,384]{2,1,0:T(8,128)(2,1)S(1)}, u32[]{:S(2)}, u32[]{:S(2)}) async-start(bf16[4,16,384]{2,1,0:T(8,128)(2,1)} %copy_bitcast_fusion), calls=%async_computation.9 | async-start | bytes 98304 | tf_op jit(solution)/shard_map/all_to_all | solution.py:156
  121.5 80.1 %copy-start.9 = (bf16[4,16,384]{2,1,0:T(8,128)(2,1)S(1)}, bf16[4,16,384]{2,1,0:T(8,128)(2,1)}, u32[]{:S(2)}) copy-start(bf16[4,16,384]{2,1,0:T(8,128)(2,1)} %copy-done.8) | copy-start | bytes 147460
  127.2 12.3 %all-to-all-start.7 = ((bf16[4,128,384]{2,1,0:T(8,128)(2,1)}), bf16[4,128,384]{2,1,0:T(8,128)(2,1)S(1)}, u32[]{:S(2)}, u32[]{:S(2)}) async-start(bf16[4,128,384]{2,1,0:T(8,128)(2,1)} %bitcast.38), calls=%async_computation.7 | async-start | bytes 786432 | tf_op jit(solution)/shard_map/all_to_all | solution.py:154
  139.6 17.8 %all-to-all-start.8 = ((bf16[4,128,384]{1,2,0:T(8,128)(2,1)}), bf16[4,128,384]{1,2,0:T(8,128)(2,1)S(1)}, u32[]{:S(2)}, u32[]{:S(2)}) async-start(bf16[4,128,384]{1,2,0:T(8,128)(2,1)} %copy.115), calls=%async_computation.8 | async-start | bytes 786432 | tf_op jit(solution)/shard_map/all_to_all | solution.py:155
  157.4 48.3 %all-to-all-start.6 = ((bf16[4,128,384]{1,2,0:T(8,128)(2,1)}), bf16[4,128,384]{1,2,0:T(8,128)(2,1)S(1)}, u32[]{:S(2)}, u32[]{:S(2)}) async-start(bf16[4,128,384]{1,2,0:T(8,128)(2,1)} %bitcast.27), calls=%async_computation.6 | async-start | bytes 786432 | tf_op jit(solution)/shard_map/all_to_all | solution.py:153
  (3 other events, 2.6 us)
where the time goes:
time: 208 us; the launch traced here: 207 us
  waiting for transfers between devices  53.8 us (26%)
  starting transfers between devices  47.8 us (23%)
  blocking collectives  40.7 us (20%)
  local copies, waits for them, and re-layouts  30.2 us (15%)
  other arithmetic  22.3 us (11%)
  matrix products  10.6 us (5%)
    psum x1, blocking collectives, local(): gain_q, gain_k = lax.psum((dq_gain, dk_gain), ('dp', 'seq'))  40.7 us
    unnamed x53, local copies, waits for them, and re-layouts  11.5 us
    all_to_all x1, waiting for transfers between devices, local(): lax.all_to_all(returned[2], 'seq', split_axis=0, concat_axis=1, tiled=True)  11.2 us
    all_to_all x1, waiting for transfers between devices, local(): lax.all_to_all(image_q, 'seq', split_axis=1, concat_axis=0, tiled=True)  8.56 us
    all_to_all x1, waiting for transfers between devices, local(): lax.all_to_all(returned[1], 'seq', split_axis=0, concat_axis=1, tiled=True)  7.73 us
    reduce_sum x1, other arithmetic, group_back(): log_total = jnp.log(jnp.sum(jnp.exp(shifted), axis=-1, keepdims=True))  7 us
    sub x1, other arithmetic, group_back(): shifted = scores - row_max  6.39 us
    all_to_all x1, starting transfers between devices, local(): lax.all_to_all(text_q, 'seq', split_axis=1, concat_axis=0, tiled=True)  6.35 us
  transfers between devices with their start and end apart: 12, of which 10 were waited for; matrix products, arithmetic and copies ran while one was open for 19% of the time, Pallas kernels for 0%

commit v1 on v0

v1 whole, which is shorter than its diff:
```python
import functools

import jax
import jax.numpy as jnp
from jax import lax
from jax.experimental import pallas as pl
from jax.experimental.pallas import tpu as pltpu
from jax.sharding import PartitionSpec as P

MESH = pl.DeviceIdType.MESH
HEAD_DIM = 128
EPSILON = 1e-06
F32 = jnp.float32
BF16 = jnp.bfloat16


def dot(a, b, contract):
    return lax.dot_general(a, b, ((contract[:1], contract[1:]), ((), ())), preferred_element_type=F32)


def inverse_rms(values):
    return lax.rsqrt(jnp.mean(values * values, axis=-1, keepdims=True) + EPSILON)


def norm_back(values, inverse, gain, upstream):
    unit = values * inverse
    lifted = upstream * gain
    mean = jnp.mean(lifted * unit, axis=-1, keepdims=True)
    return inverse * (lifted - unit * mean), upstream * unit


def partners(me, n):
    if n == 4:
        return [lax.rem(me + 2, n), 3 - me, me + 1 - 2 * lax.rem(me, 2)]
    return [lax.rem(me + step, n) for step in range(1, n)]


def kernel(
    n, dp, heads,
    iq, ik, iv, idt, tq, tk, tv, td, q_gain, k_gain,
    o_iq, o_ik, o_iv, o_tq, o_tk, o_tv, o_gain,
    qbuf, kbuf, vbuf, dbuf, knb, dka, dva, gq, gk, gv, gsum, dpbuf, sqbuf,
    fs, fr, bs, br, ls, gs, gr,
):
    me = lax.axis_index("seq")
    my_dp = lax.axis_index("dp")
    img, txt, text = iq.shape[0], tq.shape[0], tk.shape[0]
    block = img + txt
    image = img * n
    others = partners(me, n)

    def col(owner, h):
        return pl.ds(pl.multiple_of((owner * heads + h) * HEAD_DIM, HEAD_DIM), HEAD_DIM)

    def rows(start, size, unit):
        return pl.ds(pl.multiple_of(start, unit), size)

    barrier = pltpu.get_barrier_semaphore()
    for other in others:
        pl.semaphore_signal(barrier, inc=1, device_id={"seq": other}, device_id_type=MESH)

    def greet(step, carry):
        pl.semaphore_signal(
            barrier, inc=1, device_id={"dp": lax.rem(my_dp + step, dp)}, device_id_type=MESH
        )
        return carry

    lax.fori_loop(1, dp, greet, 0)
    pl.semaphore_wait(barrier, n - 1 + dp - 1)

    def forward_parts(h, source):
        return (
            (iq, qbuf.at[h, rows(source * block, img, 16)]),
            (ik, kbuf.at[h, rows(source * img, img, 16)]),
            (iv, vbuf.at[h, rows(source * img, img, 16)]),
            (idt, dbuf.at[h, rows(source * block, img, 16)]),
            (tq, qbuf.at[h, rows(source * block + img, txt, 16)]),
            (td, dbuf.at[h, rows(source * block + img, txt, 16)]),
        )

    def forward_copy(part, h, source, target):
        src, dst = forward_parts(h, source)[part]
        return pltpu.make_async_remote_copy(
            src_ref=src.at[:, col(target, h)], dst_ref=dst,
            send_sem=fs.at[part, h, target], recv_sem=fr.at[part, h, source],
            device_id={"seq": target}, device_id_type=MESH,
        )

    def send_head(h, carry):
        for other in others:
            for part in range(6):
                forward_copy(part, h, me, other).start()
        return carry

    lax.fori_loop(0, heads, send_head, 0)

    def own_head(h, carry):
        for src, dst in forward_parts(h, me):
            dst[...] = src[:, col(me, h)]
        kbuf[h, image:image + text] = tk[:, col(me, h)]
        vbuf[h, image:image + text] = tv[:, col(me, h)]
        return carry

    lax.fori_loop(0, heads, own_head, 0)
    gsum[...] = jnp.zeros_like(gsum)

    def back_parts(h, target):
        return (
            (gq.at[h, rows(target * block, img, 16)], o_iq),
            (gk.at[h, rows(target * img, img, 16)], o_ik),
            (gv.at[h, rows(target * img, img, 16)], o_iv),
            (gq.at[h, rows(target * block + img, txt, 16)], o_tq),
            (gk.at[h, rows(image + target * txt, txt, 16)], o_tk),
            (gv.at[h, rows(image + target * txt, txt, 16)], o_tv),
        )

    def back_copy(part, h, source, target):
        src, dst = back_parts(h, target)[part]
        return pltpu.make_async_remote_copy(
            src_ref=src, dst_ref=dst.at[:, col(source, h)],
            send_sem=bs.at[part, h, target], recv_sem=br.at[part, h, source],
            device_id={"seq": target}, device_id_type=MESH,
        )

    qg = q_gain[...]
    kg = k_gain[...]
    scale = HEAD_DIM ** (-0.5)

    def head(h, carry):
        for other in others:
            for part in range(6):
                forward_copy(part, h, other, me).wait_recv()
        key_src = kbuf[h].astype(F32)
        key_inv = inverse_rms(key_src)
        knb[...] = (key_src * key_inv * kg).astype(BF16)
        dka[...] = jnp.zeros_like(dka)
        dva[...] = jnp.zeros_like(dva)

        def one_block(j, inner):
            here = rows(j * block, block, 16)
            query_src = qbuf[h, here].astype(F32)
            query_inv = inverse_rms(query_src)
            qn = (query_src * query_inv * qg).astype(BF16)
            kn = knb[...]
            value = vbuf[h]
            dout = dbuf[h, here]
            scores = dot(qn, kn, (1, 1)) * scale
            exps = jnp.exp(scores - jnp.max(scores, axis=-1, keepdims=True))
            prob = exps * (1.0 / jnp.sum(exps, axis=-1, keepdims=True))
            prob_b = prob.astype(BF16)
            output = dot(prob_b, value, (1, 0)).astype(BF16)
            dprob = dot(dout, value, (1, 1))
            delta = jnp.sum(dout.astype(F32) * output.astype(F32), axis=-1, keepdims=True)
            dscore = (prob * (dprob - delta) * scale).astype(BF16)
            dqn = dot(dscore, kn, (1, 0))
            dka[...] += dot(dscore, qn, (0, 0)).astype(BF16).astype(F32)
            dva[...] += dot(prob_b, dout, (0, 0)).astype(BF16).astype(F32)
            dq, term = norm_back(query_src, query_inv, qg, dqn)
            gq[h, here] = dq.astype(BF16)
            gsum[0:1, :] += jnp.sum(term, axis=0, keepdims=True)
            return inner

        lax.fori_loop(0, n, one_block, 0)
        gv[h] = dva[...].astype(BF16)
        dk, term = norm_back(key_src, key_inv, kg, dka[...])
        gk[h] = dk.astype(BF16)
        gsum[1:2, :] += jnp.sum(term, axis=0, keepdims=True)
        for other in others:
            for part in range(6):
                back_copy(part, h, me, other).start()
        for part, (src, dst) in enumerate(back_parts(h, me)):
            pltpu.make_async_copy(src, dst.at[:, col(me, h)], ls.at[part, h]).start()
        return carry

    lax.fori_loop(0, heads, head, 0)

    dpbuf[my_dp] = gsum[...]

    def dp_copy(target):
        return pltpu.make_async_remote_copy(
            src_ref=dpbuf.at[my_dp], dst_ref=dpbuf.at[my_dp], send_sem=gs.at[0], recv_sem=gr.at[0],
            device_id={"dp": target}, device_id_type=MESH,
        )

    def dp_send(step, carry):
        dp_copy(lax.rem(my_dp + step, dp)).start()
        return carry

    lax.fori_loop(1, dp, dp_send, 0)
    rest = dpbuf.at[pl.ds(0, dp - 1)]
    pltpu.make_async_copy(rest, rest, gr.at[0]).wait()
    pltpu.make_async_copy(rest, rest, gs.at[0]).wait()
    sqbuf[me] = jnp.sum(dpbuf[...], axis=0)
    for other in others:
        pltpu.make_async_remote_copy(
            src_ref=sqbuf.at[me], dst_ref=sqbuf.at[me], send_sem=gs.at[1], recv_sem=gr.at[1],
            device_id={"seq": other}, device_id_type=MESH,
        ).start()

    def drain(h, carry):
        for part, (src, dst) in enumerate(back_parts(h, me)):
            pltpu.make_async_copy(src, dst.at[:, col(me, h)], ls.at[part, h]).wait()
        for other in others:
            for part in range(6):
                forward_copy(part, h, me, other).wait_send()
                back_copy(part, h, me, other).wait_send()
                back_copy(part, h, other, me).wait_recv()
        return carry

    lax.fori_loop(0, heads, drain, 0)
    rest = sqbuf.at[pl.ds(0, n - 1)]
    pltpu.make_async_copy(rest, rest, gr.at[1]).wait()
    pltpu.make_async_copy(rest, rest, gs.at[1]).wait()
    o_gain[...] = jnp.sum(sqbuf[...], axis=0)


def local(n, dp, iq, ik, iv, idt, tq, tk, tv, td, q_gain, k_gain):
    img, width = iq.shape[1:]
    txt, text = tq.shape[1], tk.shape[1]
    heads = width // HEAD_DIM // n
    keys = img * n + text
    queries = (img + txt) * n
    vmem = pl.BlockSpec(memory_space=pltpu.VMEM)
    out = pl.pallas_call(
        functools.partial(kernel, n, dp, heads),
        out_shape=(
            jax.ShapeDtypeStruct((img, width), BF16),
            jax.ShapeDtypeStruct((img, width), BF16),
            jax.ShapeDtypeStruct((img, width), BF16),
            jax.ShapeDtypeStruct((txt, width), BF16),
            jax.ShapeDtypeStruct((txt, width), BF16),
            jax.ShapeDtypeStruct((txt, width), BF16),
            jax.ShapeDtypeStruct((2, HEAD_DIM), F32),
        ),
        in_specs=[vmem] * 10,
        out_specs=(vmem,) * 7,
        scratch_shapes=[
            pltpu.VMEM((heads, queries, HEAD_DIM), BF16),
            pltpu.VMEM((heads, keys, HEAD_DIM), BF16),
            pltpu.VMEM((heads, keys, HEAD_DIM), BF16),
            pltpu.VMEM((heads, queries, HEAD_DIM), BF16),
            pltpu.VMEM((keys, HEAD_DIM), BF16),
            pltpu.VMEM((keys, HEAD_DIM), F32),
            pltpu.VMEM((keys, HEAD_DIM), F32),
            pltpu.VMEM((heads, queries, HEAD_DIM), BF16),
            pltpu.VMEM((heads, keys, HEAD_DIM), BF16),
            pltpu.VMEM((heads, keys, HEAD_DIM), BF16),
            pltpu.VMEM((2, HEAD_DIM), F32),
            pltpu.VMEM((dp, 2, HEAD_DIM), F32),
            pltpu.VMEM((n, 2, HEAD_DIM), F32),
            pltpu.SemaphoreType.DMA((6, heads, n)),
            pltpu.SemaphoreType.DMA((6, heads, n)),
            pltpu.SemaphoreType.DMA((6, heads, n)),
            pltpu.SemaphoreType.DMA((6, heads, n)),
            pltpu.SemaphoreType.DMA((6, heads)),
            pltpu.SemaphoreType.DMA((2,)),
            pltpu.SemaphoreType.DMA((2,)),
        ],
        compiler_params=pltpu.CompilerParams(collective_id=0, has_side_effects=True),
    )(
        iq[0], ik[0], iv[0], idt[0], tq[0], tk[0], tv[0], td[0],
        q_gain.reshape(1, HEAD_DIM), k_gain.reshape(1, HEAD_DIM),
    )
    return (*(grad[None] for grad in out[:6]), out[6][0], out[6][1])


def solution(mesh):
    split = P("dp", "seq", None)
    whole = P("dp", None, None)
    return jax.shard_map(
        functools.partial(local, mesh.shape["seq"], mesh.shape["dp"]),
        mesh=mesh,
        in_specs=(split, split, split, split, split, whole, whole, split, P(), P()),
        out_specs=(split,) * 6 + (P(), P()),
        check_vma=False,
    )
```

time: 208 us -> 85.6 us (0.41)
  Pallas kernels: 0 us -> 77.4 us
  waiting for transfers between devices: 53.8 us -> 0 us
  starting transfers between devices: 47.8 us -> 0 us
  blocking collectives: 40.7 us -> 0 us
  local copies, waits for them, and re-layouts: 30.2 us -> 7.18 us
  other arithmetic: 22.3 us -> 0 us
  matrix products: 10.6 us -> 0 us
    pallas_call x0 -> x1, Pallas kernels: none -> 77.4 us  [local(): pl.pallas_call(functools.partial(kernel, n, dp, heads), out_shape=(jax.Sh...]
    all_to_all x12 -> x0, waiting for transfers between devices: 53.8 us -> none  [the longest x1 11.2 us: local(): lax.all_to_all(returned[2], 'seq', split_axis=0, concat_axis=1, tiled=True)]
    all_to_all x12 -> x0, starting transfers between devices: 47.8 us -> none  [the longest x1 6.35 us: local(): lax.all_to_all(text_q, 'seq', split_axis=1, concat_axis=0, tiled=True)]
    psum x1 -> x0, blocking collectives: 40.7 us -> none  [local(): gain_q, gain_k = lax.psum((dq_gain, dk_gain), ('dp', 'seq'))]
    reduce_sum x7 -> x0, other arithmetic: 10.3 us -> none  [the longest x1 7 us: group_back(): log_total = jnp.log(jnp.sum(jnp.exp(shifted), axis=-1, keepdims=True))]
    all_to_all x15 -> x0, local copies, waits for them, and re-layouts: 7.24 us -> none  [the longest x2 1.51 us: local(): lax.all_to_all(image_k, 'seq', split_axis=1, concat_axis=0, tiled=True)]
    dot_general x4 -> x0, matrix products: 6.96 us -> none  [the longest x1 2.52 us: group_back(): jnp.einsum('nhqk,khd->nqhd', dscore_b, key_b, preferred_element_type=jnp....]
    sub x1 -> x0, other arithmetic: 6.39 us -> none  [group_back(): shifted = scores - row_max]
  transfers between devices with their start and end apart: 12 -> 0, of which waited for: 10 -> 0; matrix products, arithmetic and copies ran while one was open for 19% -> 0% of each run, Pallas kernels for 0% -> 0%
where the time goes in v1:
time: 85.6 us; the launch traced here: 85.2 us
  Pallas kernels  77.4 us (90%)
  local copies, waits for them, and re-layouts  7.18 us (8%)
    pallas_call x1, Pallas kernels, local(): pl.pallas_call(functools.partial(kernel, n, dp, heads), out_shape=(jax.Sh...  77.4 us
    unnamed x18, local copies, waits for them, and re-layouts  6.67 us

profile of v1, /device:TPU:0, one launch (start us, length us, event | category | flops | bytes accessed | tf_op | source)
XLA Modules:
  0.0 85.2 jit_solution(9824214052515277687)
XLA Ops:
  0.6 77.4 %shard_map.161 = (bf16[128,1536]{1,0:T(8,128)(2,1)}, bf16[128,1536]{1,0:T(8,128)(2,1)}, bf16[128,1536]{1,0:T(8,128)(2,1)}, bf16[16,1536]{1,0:T(8,128)(2,1)}, bf1...) custom-call(bf16[128,1536]{1,0:T(8,128)(2,1)} %bitcast.20, bf16[128,1536]{1,0:T(8,128)(2,1)} %bitcast.21, ...), custom_call_target="tpu_custom_call" | custom-call | tf_op jit(solution)/shard_map/pallas_call | solution.py:224
  78.0 0.0 copy-start.5
  78.0 0.7 copy-done.5
  78.7 0.5 slice_bitcast_fusion
  79.2 0.0 copy-start.1
  79.2 1.8 %copy.24 = bf16[1,128,1536]{2,1,0:T(8,128)(2,1)} copy(bf16[1,128,1536]{2,1,0:T(8,128)(2,1)} %bitcast.26) | data formatting | bytes 786432
  81.0 0.0 copy-done.1
  81.0 0.0 copy-start
  81.0 0.7 copy.25
  81.8 0.4 copy-done
  82.2 0.0 copy-start.4
  82.2 0.7 copy.26
  82.9 0.1 copy-done.4
  83.0 0.0 copy-start.3
  83.0 0.6 copy.27
  83.6 0.2 copy-done.3
  83.8 0.0 copy-start.2
  83.8 0.6 copy.28
  84.4 0.2 copy-done.2
  84.6 0.6 copy.29
Async XLA Ops:
  78.0 0.7 copy-start.5
  79.2 1.8 %copy-start.1 = (bf16[128,1536]{1,0:T(8,128)(2,1)S(1)}, bf16[128,1536]{1,0:T(8,128)(2,1)}, u32[]{:S(2)}) copy-start(bf16[128,1536]{1,0:T(8,128)(2,1)} %get-tuple-element.16) | copy-start | bytes 1179652
  81.0 1.1 %copy-start = (bf16[128,1536]{1,0:T(8,128)(2,1)S(1)}, bf16[128,1536]{1,0:T(8,128)(2,1)}, u32[]{:S(2)}) copy-start(bf16[128,1536]{1,0:T(8,128)(2,1)} %get-tuple-element.17) | copy-start | bytes 1179652
  82.2 0.8 copy-start.4
  83.0 0.8 copy-start.3
  83.8 0.8 copy-start.2

commit v2 on v1

--- a/solution.py
+++ b/solution.py
@@ -37,10 +37,11 @@
 
 def kernel(
     n, dp, heads,
-    iq, ik, iv, idt, tq, tk, tv, td, q_gain, k_gain,
-    o_iq, o_ik, o_iv, o_tq, o_tk, o_tv, o_gain,
+    h_iq, h_ik, h_iv, h_idt, h_tq, h_tk, h_tv, h_td, q_gain, k_gain,
+    o_iq, o_ik, o_iv, o_tq, o_tk, o_tv, o_qg, o_kg,
+    iq, ik, iv, idt, tq, tk, tv, td,
     qbuf, kbuf, vbuf, dbuf, knb, dka, dva, gq, gk, gv, gsum, dpbuf, sqbuf,
-    fs, fr, bs, br, ls, gs, gr,
+    fs, fr, bs, br, ls, gs, gr, ins,
 ):
     me = lax.axis_index("seq")
     my_dp = lax.axis_index("dp")
@@ -55,6 +56,17 @@
     def rows(start, size, unit):
         return pl.ds(pl.multiple_of(start, unit), size)
 
+    loads = [
+        pltpu.make_async_copy(src, dst, ins.at[i])
+        for i, (src, dst) in enumerate(
+            zip(
+                (h_iq, h_ik, h_iv, h_idt, h_tq, h_td, h_tk, h_tv),
+                (iq, ik, iv, idt, tq, td, tk, tv),
+            )
+        )
+    ]
+    for load in loads:
+        load.start()
     barrier = pltpu.get_barrier_semaphore()
     for other in others:
         pl.semaphore_signal(barrier, inc=1, device_id={"seq": other}, device_id_type=MESH)
@@ -67,6 +79,8 @@
 
     lax.fori_loop(1, dp, greet, 0)
     pl.semaphore_wait(barrier, n - 1 + dp - 1)
+    for load in loads:
+        load.wait()
 
     def forward_parts(h, source):
         return (
@@ -211,7 +225,24 @@
     rest = sqbuf.at[pl.ds(0, n - 1)]
     pltpu.make_async_copy(rest, rest, gr.at[1]).wait()
     pltpu.make_async_copy(rest, rest, gs.at[1]).wait()
-    o_gain[...] = jnp.sum(sqbuf[...], axis=0)
+    total = jnp.sum(sqbuf[...], axis=0)
+    o_qg[...] = total[0:1]
+    o_kg[...] = total[1:2]
+
+
+def hand_on(*refs):
+    count = (len(refs) - 2) // 3
+    sources, results, held = refs[:count], refs[count:2 * count], refs[2 * count:3 * count]
+    in_sem, out_sem = refs[3 * count:]
+    loads = [pltpu.make_async_copy(a, b, in_sem.at[i]) for i, (a, b) in enumerate(zip(sources, held))]
+    stores = [pltpu.make_async_copy(a, b, out_sem.at[i]) for i, (a, b) in enumerate(zip(held, results))]
+    for load in loads:
+        load.start()
+    for load, store in zip(loads, stores):
+        load.wait()
+        store.start()
+    for store in stores:
+        store.wait()
 
 
 def local(n, dp, iq, ik, iv, idt, tq, tk, tv, td, q_gain, k_gain):
@@ -221,6 +252,7 @@
     keys = img * n + text
     queries = (img + txt) * n
     vmem = pl.BlockSpec(memory_space=pltpu.VMEM)
+    hbm = pl.BlockSpec(memory_space=pl.ANY)
     out = pl.pallas_call(
         functools.partial(kernel, n, dp, heads),
         out_shape=(
@@ -230,11 +262,20 @@
             jax.ShapeDtypeStruct((txt, width), BF16),
             jax.ShapeDtypeStruct((txt, width), BF16),
             jax.ShapeDtypeStruct((txt, width), BF16),
-            jax.ShapeDtypeStruct((2, HEAD_DIM), F32),
+            jax.ShapeDtypeStruct((1, HEAD_DIM), F32),
+            jax.ShapeDtypeStruct((1, HEAD_DIM), F32),
         ),
-        in_specs=[vmem] * 10,
-        out_specs=(vmem,) * 7,
+        in_specs=[hbm] * 8 + [vmem] * 2,
+        out_specs=(hbm,) * 6 + (vmem,) * 2,
         scratch_shapes=[
+            pltpu.VMEM((img, width), BF16),
+            pltpu.VMEM((img, width), BF16),
+            pltpu.VMEM((img, width), BF16),
+            pltpu.VMEM((img, width), BF16),
+            pltpu.VMEM((txt, width), BF16),
+            pltpu.VMEM((text, width), BF16),
+            pltpu.VMEM((text, width), BF16),
+            pltpu.VMEM((txt, width), BF16),
             pltpu.VMEM((heads, queries, HEAD_DIM), BF16),
             pltpu.VMEM((heads, keys, HEAD_DIM), BF16),
             pltpu.VMEM((heads, keys, HEAD_DIM), BF16),
@@ -255,13 +296,22 @@
             pltpu.SemaphoreType.DMA((6, heads)),
             pltpu.SemaphoreType.DMA((2,)),
             pltpu.SemaphoreType.DMA((2,)),
+            pltpu.SemaphoreType.DMA((8,)),
         ],
         compiler_params=pltpu.CompilerParams(collective_id=0, has_side_effects=True),
     )(
         iq[0], ik[0], iv[0], idt[0], tq[0], tk[0], tv[0], td[0],
         q_gain.reshape(1, HEAD_DIM), k_gain.reshape(1, HEAD_DIM),
     )
-    return (*(grad[None] for grad in out[:6]), out[6][0], out[6][1])
+    final = pl.pallas_call(
+        hand_on,
+        out_shape=tuple(jax.ShapeDtypeStruct(a.shape, a.dtype) for a in out),
+        in_specs=[hbm] * 8,
+        out_specs=(hbm,) * 8,
+        scratch_shapes=[pltpu.VMEM(a.shape, a.dtype) for a in out]
+        + [pltpu.SemaphoreType.DMA((8,)), pltpu.SemaphoreType.DMA((8,))],
+    )(*out)
+    return (*(grad[None] for grad in final[:6]), final[6][0], final[7][0])
 
 
 def solution(mesh):

time: 85.6 us -> 79.1 us (0.924)
  local copies, waits for them, and re-layouts: 7.18 us -> 0 us
  Pallas kernels: 77.4 us -> 78.3 us
    unnamed x18 -> x0, local copies, waits for them, and re-layouts: 6.67 us -> none
    pallas_call x0 -> x1, Pallas kernels: none -> 2.18 us  [local(): pl.pallas_call(hand_on, out_shape=tuple((jax.ShapeDtypeStruct(a.shape, a....]
    pallas_call x1, Pallas kernels: 77.4 us -> 76.1 us  [local(): pl.pallas_call(functools.partial(kernel, n, dp, heads), out_shape=(jax.Sh...]
where the time goes in v2:
time: 79.1 us; the launch traced here: 78.9 us
  Pallas kernels  78.3 us (99%)
    pallas_call x1, Pallas kernels, local(): pl.pallas_call(functools.partial(kernel, n, dp, heads), out_shape=(jax.Sh...  76.1 us
    pallas_call x1, Pallas kernels, local(): pl.pallas_call(hand_on, out_shape=tuple((jax.ShapeDtypeStruct(a.shape, a....  2.18 us

profile of v2, /device:TPU:0, one launch (start us, length us, event | category | flops | bytes accessed | tf_op | source)
XLA Modules:
  0.0 78.9 jit_solution(17158104489505911787)
XLA Ops:
  0.6 76.1 %shard_map.161 = (bf16[128,1536]{1,0:T(8,128)(2,1)}, bf16[128,1536]{1,0:T(8,128)(2,1)}, bf16[128,1536]{1,0:T(8,128)(2,1)}, bf16[16,1536]{1,0:T(8,128)(2,1)}, bf1...) custom-call(bf16[128,1536]{1,0:T(8,128)(2,1)} %bitcast.18, ...), custom_call_target="tpu_custom_call" | custom-call | tf_op jit(solution)/shard_map/pallas_call | solution.py:256
  76.7 2.2 %shard_map.162 = (bf16[128,1536]{1,0:T(8,128)(2,1)}, bf16[128,1536]{1,0:T(8,128)(2,1)}, bf16[128,1536]{1,0:T(8,128)(2,1)}, bf16[16,1536]{1,0:T(8,128)(2,1)}, bf1...) custom-call(bf16[128,1536]{1,0:T(8,128)(2,1)} %get-tuple-element.24.refs_0_, ...), custom_call_target="tpu_custom_call" | custom-call | tf_op jit(solution)/shard_map/pallas_call | solution.py:306

commit v3 on v2

--- a/solution.py
+++ b/solution.py
@@ -135,6 +135,13 @@
             send_sem=bs.at[part, h, target], recv_sem=br.at[part, h, source],
             device_id={"seq": target}, device_id_type=MESH,
         )
+
+    def send_back(h):
+        for other in others:
+            for part in range(6):
+                back_copy(part, h, me, other).start()
+        for part, (src, dst) in enumerate(back_parts(h, me)):
+            pltpu.make_async_copy(src, dst.at[:, col(me, h)], ls.at[part, h]).start()
 
     qg = q_gain[...]
     kg = k_gain[...]
@@ -179,11 +186,11 @@
         dk, term = norm_back(key_src, key_inv, kg, dka[...])
         gk[h] = dk.astype(BF16)
         gsum[1:2, :] += jnp.sum(term, axis=0, keepdims=True)
-        for other in others:
-            for part in range(6):
-                back_copy(part, h, me, other).start()
-        for part, (src, dst) in enumerate(back_parts(h, me)):
-            pltpu.make_async_copy(src, dst.at[:, col(me, h)], ls.at[part, h]).start()
+
+        @pl.when(h < heads - 1)
+        def _():
+            send_back(h)
+
         return carry
 
     lax.fori_loop(0, heads, head, 0)
@@ -210,6 +217,7 @@
             src_ref=sqbuf.at[me], dst_ref=sqbuf.at[me], send_sem=gs.at[1], recv_sem=gr.at[1],
             device_id={"seq": other}, device_id_type=MESH,
         ).start()
+    send_back(heads - 1)
 
     def drain(h, carry):
         for part, (src, dst) in enumerate(back_parts(h, me)):

time: 79.1 us -> 77.5 us (0.980)
  Pallas kernels: 78.3 us -> 76.6 us
    pallas_call x1, Pallas kernels: 76.1 us -> 74.5 us  [local(): pl.pallas_call(functools.partial(kernel, n, dp, heads), out_shape=(jax.Sh...]
where the time goes in v3:
time: 77.5 us; the launch traced here: 77.3 us
  Pallas kernels  76.6 us (99%)
    pallas_call x1, Pallas kernels, local(): pl.pallas_call(functools.partial(kernel, n, dp, heads), out_shape=(jax.Sh...  74.5 us
    pallas_call x1, Pallas kernels, local(): pl.pallas_call(hand_on, out_shape=tuple((jax.ShapeDtypeStruct(a.shape, a....  2.18 us

profile of v3, /device:TPU:0, one launch (start us, length us, event | category | flops | bytes accessed | tf_op | source)
XLA Modules:
  0.0 77.3 jit_solution(13131000317715789766)
XLA Ops:
  0.6 74.5 %shard_map.161 = (bf16[128,1536]{1,0:T(8,128)(2,1)}, bf16[128,1536]{1,0:T(8,128)(2,1)}, bf16[128,1536]{1,0:T(8,128)(2,1)}, bf16[16,1536]{1,0:T(8,128)(2,1)}, bf1...) custom-call(bf16[128,1536]{1,0:T(8,128)(2,1)} %bitcast.18, ...), custom_call_target="tpu_custom_call" | custom-call | tf_op jit(solution)/shard_map/pallas_call | solution.py:264
  75.1 2.2 %shard_map.162 = (bf16[128,1536]{1,0:T(8,128)(2,1)}, bf16[128,1536]{1,0:T(8,128)(2,1)}, bf16[128,1536]{1,0:T(8,128)(2,1)}, bf16[16,1536]{1,0:T(8,128)(2,1)}, bf1...) custom-call(bf16[128,1536]{1,0:T(8,128)(2,1)} %get-tuple-element.24.refs_0_, ...), custom_call_target="tpu_custom_call" | custom-call | tf_op jit(solution)/shard_map/pallas_call | solution.py:314
